TPU v7x, 128 devices: a whole 4x4x4 slice. The times are simulated.
128 devices in a mesh: space: 8 (over z_lo, x), mode: 16 (over z_hi, y, core).
Axes of the slice: x: 4, y: 4, z: 4 (z_hi: 2, z_lo: 2; z = z_hi * 2 + z_lo), core: 2. Of those that a mesh axis runs over, the one named last changes fastest.
Arguments:
- excess_phonon_enthalpy: bfloat16 [768, 64, 128, 128], P('mode', 'space'), may hold values from -0.21972656 to 0.21972656
- thermal_offset: float32 [128, 128, 64], P('space', 'mode'), may hold values from -6 to 6
- state_specific_warmth_scaled: float32 [768], P('mode'), may hold values from 0.5 to 2
- scattering_lifetimes: float32 [768], P('mode'), may hold values from 0.5 to 50
- state_polarization_label: int32 [768], P('mode'), may hold values from 0 to 5
- state_orientation_label: int32 [768], P('mode'), may hold values from 0 to 15
- polarization_propagation_rate: float32 [6], replicated, may hold values from 0.3 to 1
- thermal_conductance_bulk: float32 [128, 128, 64], P('space', 'mode'), may hold values from 0.25 to 1
- substance_label: int32 [128, 128, 64], P('space', 'mode'), may hold values 0 or 1
Outputs:
- final_temperature: float32 [128, 128, 64], P('space', 'mode')
- heat_flux: float32 [3, 128, 128, 64], P(None, 'space', 'mode')
Inputs may be any that keep to these rules, and one draw needn't show every extreme that they name: `substance_label`: 1 marks a pore cell.
All inputs are finite; a program needn't handle non-finite values. No bound on the sum of `substance_label` on one device may be relied on, other than what follows from the above.
Results may differ from a plain program's by a relative error of at most 0.0028.
Values may be sent and summed in bfloat16 or wider, within the bound.
No kernel may reach another device: no remote copies, remote signals or barrier semaphores. Data moves between devices by JAX's collectives and lax.ppermute only.
A program may use at most 128 MiB of HBM per device.

v0:
```python
import math
import jax
import jax.numpy as jnp
from jax import lax
from jax.sharding import PartitionSpec as P

M = 768
SWEEPS = 4
OUTER = 2
time_step = 0.25
pore_factor = 0.1
kappa_top = 1.0


def padded_2(cells, sides, width):
    for axis, dim in sides:
        count = lax.axis_size(axis)
        ends = count - 1
        head = lax.slice_in_dim(cells, 0, width, axis=dim)
        tail = lax.slice_in_dim(cells, cells.shape[dim] - width, cells.shape[dim], axis=dim)
        cells = jnp.concatenate(
            [
                lax.ppermute(tail, axis, [(i, (i + 1) % count) for i in range(ends)]),
                cells,
                lax.ppermute(head, axis, [((i + 1) % count, i) for i in range(ends)]),
            ],
            axis=dim,
        )
    return cells


def sent_to_all(shard, axis):
    copies = jnp.broadcast_to(shard, (lax.axis_size(axis), *shard.shape))
    return lax.all_to_all(copies, axis, split_axis=0, concat_axis=0, tiled=True)


def over_copies(shard, axis):
    everything = sent_to_all(shard, axis)
    return jnp.sum(everything, axis=0)


def in_blocks(shard, dim, length):
    before, after = (shard.shape[:dim], shard.shape[dim + 1 :])
    return jnp.moveaxis(shard.reshape(*before, length, -1, *after), dim, 0)


def sum_at_owner(shard, axis, dim):
    length = lax.axis_size(axis)
    pieces = lax.all_to_all(in_blocks(shard, dim, length), axis, 0, 0, tiled=True)
    return jnp.sum(pieces, axis=0)


def mode_table(
    state_polarization_label,
    state_orientation_label,
    state_specific_warmth_scaled,
    scattering_lifetimes,
    polarization_propagation_rate,
):
    branches = jnp.arange(polarization_propagation_rate.shape[0], dtype=jnp.int32)
    onehot = (state_polarization_label[:, None] == branches[None, :]).astype(jnp.float32)
    speed = jnp.sum(onehot * polarization_propagation_rate[None, :], axis=1)
    polar = state_orientation_label // 4
    azimuth = state_orientation_label % 4
    cosine = (2 * polar + 1).astype(jnp.float32) * 0.25 - 1.0
    sine = jnp.sqrt(1.0 - cosine * cosine)
    angle = (azimuth.astype(jnp.float32) + 0.5) * (math.pi / 2.0)
    velocity = (speed * sine * jnp.cos(angle), speed * sine * jnp.sin(angle), speed * cosine)
    rates = 1.0 / scattering_lifetimes
    capacity = state_specific_warmth_scaled / float(M)
    return (velocity, rates, capacity)


def upwind(padded, temp_slab, along_x, along_y, along_z, rates, capacity):

    def widen(values):
        return values[:, None, None, None]

    current = padded[:, 1:-1]
    z_before = padded[:, :-2]
    z_after = padded[:, 2:]
    x_padded = jnp.pad(current, ((0, 0), (0, 0), (1, 1), (0, 0)))
    y_padded = jnp.pad(current, ((0, 0), (0, 0), (0, 0), (1, 1)))

    def advect(speed, before, after):
        flow = widen(speed)
        return jnp.maximum(flow, 0.0) * (current - before) + jnp.minimum(flow, 0.0) * (
            after - current
        )

    total_advect = advect(along_x, x_padded[:, :, :-2], x_padded[:, :, 2:])
    total_advect = total_advect + advect(along_y, y_padded[:, :, :, :-2], y_padded[:, :, :, 2:])
    total_advect = total_advect + advect(along_z, z_before, z_after)
    updated = (
        current
        - time_step * total_advect
        + time_step * widen(rates) * (widen(capacity) * temp_slab[None] - current)
    )
    weights = jnp.stack([rates, along_x, along_y, along_z])
    moments = jnp.einsum("km,mzxy->kzxy", weights, updated, precision=lax.Precision.HIGHEST)
    return (updated, moments)


def harmonic(first, second):
    summed = first + second
    positive = summed > 0.0
    return jnp.where(positive, 2.0 * first * second / jnp.where(positive, summed, 1.0), 0.0)


def face_table(kappa_ext):
    center = kappa_ext[1:-1, 1:-1]
    z_padded = jnp.pad(center, ((0, 0), (0, 0), (1, 1)))
    return (
        harmonic(center, kappa_ext[2:, 1:-1]),
        harmonic(kappa_ext[:-2, 1:-1], center),
        harmonic(center, kappa_ext[1:-1, 2:]),
        harmonic(kappa_ext[1:-1, :-2], center),
        harmonic(center, z_padded[:, :, 2:]),
        harmonic(z_padded[:, :, :-2], center),
    )


def crop(values, matrix_height, matrix_breadth):
    top = (values.shape[0] - matrix_height) // 2
    left = (values.shape[1] - matrix_breadth) // 2
    return values[top : top + matrix_height, left : left + matrix_breadth]


def apply_operator(padded, faces, total):
    matrix_height = padded.shape[0] - 2
    matrix_breadth = padded.shape[1] - 2
    cut = [crop(face, matrix_height, matrix_breadth) for face in faces]
    center = padded[1:-1, 1:-1]
    z_padded = jnp.pad(center, ((0, 0), (0, 0), (1, 1)))
    spread = cut[0] * (padded[2:, 1:-1] - center) + cut[1] * (padded[:-2, 1:-1] - center)
    spread = spread + cut[2] * (padded[1:-1, 2:] - center) + cut[3] * (padded[1:-1, :-2] - center)
    spread = (
        spread + cut[4] * (z_padded[:, :, 2:] - center) + cut[5] * (z_padded[:, :, :-2] - center)
    )
    return total * center - spread


def divergence(fluxes):
    z_flux = jnp.pad(fluxes[2][1:-1, 1:-1], ((0, 0), (0, 0), (1, 1)))
    summed = (
        fluxes[0][2:, 1:-1] - fluxes[0][:-2, 1:-1] + (fluxes[1][1:-1, 2:] - fluxes[1][1:-1, :-2])
    )
    summed = summed + (z_flux[:, :, 2:] - z_flux[:, :, :-2])
    return summed * 0.5


def chebyshev(rhs, faces, total, extend, matrix_height, matrix_breadth):
    theta = total + 6.0 * kappa_top
    spread = 6.0 * kappa_top
    sigma = theta / spread
    rho = 1.0 / sigma
    residual = rhs
    direction = rhs / theta
    correction = jnp.zeros((matrix_height, matrix_breadth, rhs.shape[2]), jnp.float32)
    for sweep in range(SWEEPS):
        correction = correction + crop(direction, matrix_height, matrix_breadth)
        if sweep < SWEEPS - 1:
            image = apply_operator(extend(direction), faces, total)
            residual = crop(residual, image.shape[0], image.shape[1]) - image
            rho_next = 1.0 / (2.0 * sigma - rho)
            direction = (
                rho_next * rho * crop(direction, image.shape[0], image.shape[1])
                + 2.0 * rho_next / spread * residual
            )
            rho = rho_next
    return correction


def unchanged(direction):
    return direction


def to_slab(block):
    upright = jnp.transpose(block, (2, 0, 1))
    moved = lax.all_to_all(upright, "space", split_axis=0, concat_axis=1, tiled=True)
    return lax.all_gather(moved, "mode", axis=2, tiled=True)


def kinetic(state, temp_slab, velocity, rates, capacity):
    padded = padded_2(state, (("space", 1),), 1)
    local = padded.shape[0]
    group = math.gcd(local, 8)
    count = local // group
    shaped = padded.reshape((count, group) + padded.shape[1:])
    params = (
        velocity[0].reshape(count, group),
        velocity[1].reshape(count, group),
        velocity[2].reshape(count, group),
        rates.reshape(count, group),
        capacity.reshape(count, group),
    )

    def step(carry, inputs):
        block, along_x, along_y, along_z, rate_part, cap_part = inputs
        updated, moments = upwind(
            block.astype(jnp.float32), temp_slab, along_x, along_y, along_z, rate_part, cap_part
        )
        return (carry + moments, updated.astype(jnp.bfloat16))

    start = jnp.zeros((4,) + state.shape[1:], jnp.float32)
    moments, news = lax.scan(step, start, (shaped,) + params)
    return (news.reshape(state.shape), moments)


def per_device(
    excess_phonon_enthalpy,
    thermal_offset,
    state_specific_warmth_scaled,
    scattering_lifetimes,
    state_polarization_label,
    state_orientation_label,
    polarization_propagation_rate,
    thermal_conductance_bulk,
    substance_label,
):
    velocity, rates, capacity = mode_table(
        state_polarization_label,
        state_orientation_label,
        state_specific_warmth_scaled,
        scattering_lifetimes,
        polarization_propagation_rate,
    )
    total = over_copies(jnp.sum(capacity * rates), "mode")
    kappa = thermal_conductance_bulk * jnp.where(substance_label == 1, pore_factor, 1.0)
    matrix_height = thermal_offset.shape[0]
    matrix_breadth = thermal_offset.shape[1]
    kappa_ext = padded_2(kappa.astype(jnp.bfloat16), (("space", 0), ("mode", 1)), SWEEPS).astype(
        kappa.dtype
    )
    faces = face_table(kappa_ext)
    spatial_entries = thermal_offset
    state = excess_phonon_enthalpy
    fluxes = None
    for outer in range(OUTER):
        temp_slab = to_slab(spatial_entries)
        state, moments = kinetic(state, temp_slab, velocity, rates, capacity)
        reduced = sum_at_owner(moments, "mode", 3)
        summed = lax.all_to_all(reduced, "space", split_axis=2, concat_axis=1, tiled=True)
        blocks = jnp.transpose(summed, (0, 2, 3, 1))
        fluxes = blocks[1:]
        flux_ext = padded_2(
            fluxes.astype(jnp.bfloat16), (("space", 1), ("mode", 2)), SWEEPS
        ).astype(fluxes.dtype)
        rhs = -divergence(flux_ext)
        correction = chebyshev(rhs, faces, total, unchanged, matrix_height, matrix_breadth)
        spatial_entries = blocks[0] / total + correction
    return (spatial_entries, fluxes)


def solution(mesh):
    placed = (
        P("mode", "space", None, None),
        P("space", "mode", None),
        P("mode"),
        P("mode"),
        P("mode"),
        P("mode"),
        P(),
        P("space", "mode", None),
        P("space", "mode", None),
    )
    return jax.shard_map(
        per_device,
        mesh=mesh,
        in_specs=placed,
        out_specs=(P("space", "mode", None), P(None, "space", "mode", None)),
        check_vma=False,
    )
```

profile of v0, /device:TPU:31, one launch (start us, length us, event | category | flops | bytes accessed | tf_op | source)
XLA Modules:
  0.0 615.3 jit_solution(17676936092251280161)
XLA Ops:
  0.7 4.0 fusion.165
  4.7 3.4 collective-permute-start
  11.0 6.4 %all-to-all-start = ((f32[8,1,1024]{2,1,0:T(1,128)}), f32[8,1,1024]{2,1,0:T(1,128)S(1)}, u32[]{:S(2)}, u32[]{:S(2)}) async-start(f32[8,1,1024]{2,1,0:T(1,128)} %reshape.250), calls=%async_computation | async-start | bytes 65536 | tf_op jit(solution)/shard_map/all_to_all | solution.py:180
  18.7 29.0 %all-to-all-done = f32[8,1,1024]{2,1,0:T(1,128)S(1)} async-done(((f32[8,1,1024]{2,1,0:T(1,128)}), f32[8,1,1024]{2,1,0:T(1,128)S(1)}, u32[]{:S(2)}, u32[]{:S(2)}) %all-to-all-start) | async-done | bytes 32800 | tf_op jit(solution)/shard_map/all_to_all | solution.py:180
  49.0 9.2 %all-to-all-start.3 = ((f32[16,1,1]{2,1,0:T(1,128)}), f32[16,1,1]{2,1,0:T(1,128)S(1)}, u32[]{:S(2)}, u32[]{:S(2)}) async-start(f32[16,1,1]{2,1,0:T(1,128)} %broadcast_in_dim.52), calls=%async_computation.3 | async-start | bytes 16384 | tf_op jit(solution)/shard_map/all_to_all | solution.py:34
  59.9 19.9 %all_gather.6 = f32[8,128,128]{1,2,0:T(8,128)S(1)} all-gather(f32[8,128,8]{1,2,0:T(8,128)S(1)} %all_to_all.65), channel_id=1, replica_groups=mesh['space'=8,'mode'=16] {'mode'}, dimensions={2}, use_global_device_ids=true | all-gather | bytes 557056 | tf_op jit(solution)/shard_map/all_gather | solution.py:181
  80.1 13.3 %pad_maximum_fusion = bf16[48,10,128,128]{3,2,1,0:T(8,128)(2,1)} fusion(bf16[48,1,128,128]{3,2,1,0:T(8,128)(2,1)} %collective-permute-done.1, bf16[48,8,128,128]{3,2,1,0:T(8,128)(2,1)} %param.13, bf16[48,1,128,128]{3,2,1,0:T(8,128)(2,1)} %collective-permute-done), kind=kLoop, calls=%fused_computation.96 | loop fusion | flops 15728640 | bytes 31457280 | tf_op jit(solution)/shard_map/concatenate | solution.py:21
  93.3 99.1 %while.28 = (s32[]{:T(128)}, f32[4,8,128,128]{3,0,2,1:T(4,128)S(1)}, bf16[6,8,8,128,128]{4,1,3,2,0:T(8,128)(2,1)}, f32[6,8]{1,0:T(8,128)S(1)}, f32[6,8]{1,0:T(8,...) while((s32[]{:T(128)}, ...), condition=%wide.region_2.3_spmd.clone, body=%wide.region_1.2_spmd.clone.sunk | while | flops 77856920 | bytes 49284748 | solution.py:206
  97.5 5.3 bitcast_dynamic-update-slice_fusion.2
  102.8 7.0 %select_add_fusion.4 = f32[4,8,128,128]{3,0,2,1:T(4,128)S(1)} fusion(f32[4,8,128,128]{3,0,2,1:T(4,128)S(1)} %get-tuple-element.704, f32[8,8,128,128]{3,0,2,1:T(8,128)} %get-tuple-element.671, pred[]{:T(512)S(6)} %compare.22, f32[1,8]{1,0:T(1,128)S(1)} %get-tuple-element.665, f32[1,8]{1,0:T(1,128)S(1)} %get-tuple-element.667, ...), kind=kOutput, calls=%fused_computation.20.clone.1 | convolution fusion | flops 51380320 | bytes 8388737 | tf_op jit(solution)/shard_map/while/body/eval_jaxpr/km,mzxy->kzxy/dot_general | solution.py:100
  114.0 5.3 bitcast_dynamic-update-slice_fusion.2
  119.4 7.0 %select_add_fusion.4 = f32[4,8,128,128]{3,0,2,1:T(4,128)S(1)} fusion(f32[4,8,128,128]{3,0,2,1:T(4,128)S(1)} %get-tuple-element.704, f32[8,8,128,128]{3,0,2,1:T(8,128)} %get-tuple-element.671, pred[]{:T(512)S(6)} %compare.22, f32[1,8]{1,0:T(1,128)S(1)} %get-tuple-element.665, f32[1,8]{1,0:T(1,128)S(1)} %get-tuple-element.667, ...), kind=kOutput, calls=%fused_computation.20.clone.1 | convolution fusion | flops 51380320 | bytes 8388737 | tf_op jit(solution)/shard_map/while/body/eval_jaxpr/km,mzxy->kzxy/dot_general | solution.py:100
  130.6 5.4 bitcast_dynamic-update-slice_fusion.2
  135.9 7.0 %select_add_fusion.4 = f32[4,8,128,128]{3,0,2,1:T(4,128)S(1)} fusion(f32[4,8,128,128]{3,0,2,1:T(4,128)S(1)} %get-tuple-element.704, f32[8,8,128,128]{3,0,2,1:T(8,128)} %get-tuple-element.671, pred[]{:T(512)S(6)} %compare.22, f32[1,8]{1,0:T(1,128)S(1)} %get-tuple-element.665, f32[1,8]{1,0:T(1,128)S(1)} %get-tuple-element.667, ...), kind=kOutput, calls=%fused_computation.20.clone.1 | convolution fusion | flops 51380320 | bytes 8388737 | tf_op jit(solution)/shard_map/while/body/eval_jaxpr/km,mzxy->kzxy/dot_general | solution.py:100
  147.1 5.3 bitcast_dynamic-update-slice_fusion.2
  152.4 7.0 %select_add_fusion.4 = f32[4,8,128,128]{3,0,2,1:T(4,128)S(1)} fusion(f32[4,8,128,128]{3,0,2,1:T(4,128)S(1)} %get-tuple-element.704, f32[8,8,128,128]{3,0,2,1:T(8,128)} %get-tuple-element.671, pred[]{:T(512)S(6)} %compare.22, f32[1,8]{1,0:T(1,128)S(1)} %get-tuple-element.665, f32[1,8]{1,0:T(1,128)S(1)} %get-tuple-element.667, ...), kind=kOutput, calls=%fused_computation.20.clone.1 | convolution fusion | flops 51380320 | bytes 8388737 | tf_op jit(solution)/shard_map/while/body/eval_jaxpr/km,mzxy->kzxy/dot_general | solution.py:100
  163.6 5.3 bitcast_dynamic-update-slice_fusion.2
  169.0 7.0 %select_add_fusion.4 = f32[4,8,128,128]{3,0,2,1:T(4,128)S(1)} fusion(f32[4,8,128,128]{3,0,2,1:T(4,128)S(1)} %get-tuple-element.704, f32[8,8,128,128]{3,0,2,1:T(8,128)} %get-tuple-element.671, pred[]{:T(512)S(6)} %compare.22, f32[1,8]{1,0:T(1,128)S(1)} %get-tuple-element.665, f32[1,8]{1,0:T(1,128)S(1)} %get-tuple-element.667, ...), kind=kOutput, calls=%fused_computation.20.clone.1 | convolution fusion | flops 51380320 | bytes 8388737 | tf_op jit(solution)/shard_map/while/body/eval_jaxpr/km,mzxy->kzxy/dot_general | solution.py:100
  180.2 5.3 bitcast_dynamic-update-slice_fusion.2
  185.4 7.0 %select_add_fusion.4 = f32[4,8,128,128]{3,0,2,1:T(4,128)S(1)} fusion(f32[4,8,128,128]{3,0,2,1:T(4,128)S(1)} %get-tuple-element.704, f32[8,8,128,128]{3,0,2,1:T(8,128)} %get-tuple-element.671, pred[]{:T(512)S(6)} %compare.22, f32[1,8]{1,0:T(1,128)S(1)} %get-tuple-element.665, f32[1,8]{1,0:T(1,128)S(1)} %get-tuple-element.667, ...), kind=kOutput, calls=%fused_computation.20.clone.1 | convolution fusion | flops 51380320 | bytes 8388737 | tf_op jit(solution)/shard_map/while/body/eval_jaxpr/km,mzxy->kzxy/dot_general | solution.py:100
  194.3 3.3 copy.139
  197.6 9.6 %all-to-all-start.1 = ((f32[16,4,8,128,8]{3,4,2,1,0:T(8,128)}), f32[16,4,8,128,8]{3,4,2,1,0:T(8,128)S(1)}, u32[]{:S(2)}, u32[]{:S(2)}) async-start(f32[16,4,8,128,8]{3,4,2,1,0:T(8,128)} %copy.139), calls=%async_computation.1 | async-start | bytes 4194304 | tf_op jit(solution)/shard_map/all_to_all | solution.py:49
  209.1 3.5 collective-permute-start.9
  214.0 7.4 %copy.135 = bf16[6,8,8,128,128]{4,3,2,1,0:T(8,128)(2,1)S(1)} copy(bf16[6,8,8,128,128]{4,1,3,2,0:T(8,128)(2,1)} %get-tuple-element.241) | data formatting | bytes 25165824 | tf_op jit(solution)/shard_map/while | solution.py:206
  223.4 4.0 collective-permute-start.2
  229.4 4.5 all-to-all-done.1
  237.6 3.9 all-to-all-start.2
  241.6 5.9 collective-permute-start.10
  249.4 18.8 %all-to-all-done.2 = f32[8,1,4096]{2,1,0:T(1,128)S(1)} async-done(((f32[8,1,4096]{2,1,0:T(1,128)}), f32[8,1,4096]{2,1,0:T(1,128)S(1)}, u32[]{:S(2)}, u32[]{:S(2)}) %all-to-all-start.2) | async-done | bytes 131104 | tf_op jit(solution)/shard_map/all_to_all | solution.py:243
  274.7 3.4 collective-permute-start.5
  279.8 3.9 collective-permute-done.4
  284.0 3.8 collective-permute-done.5
  289.3 7.1 %collective-permute-start.6 = (bf16[3,24,4,64]{3,2,1,0:T(4,128)(2,1)S(1)}, bf16[3,24,4,64]{3,2,1,0:T(4,128)(2,1)S(1)}, u32[]{:S(2)}, u32[]{:S(2)}) collective-permute-start(bf16[3,24,4,64]{3,2,1,0:T(4,128)(2,1)S(1)} %get-tuple-element.528), channel_id=1, source_target_pairs={{0,1},{1,2},{2,3},{3,4},{4,5},{5,6},{6,7},{7,8},{8,9},{9,10},{10,1... | collective-permute-start | bytes 110600 | tf_op jit(solution)/shard_map/ppermute | solution.py:23
  298.5 3.0 compare_select_fusion.2
  301.5 3.6 copy.136
  305.1 3.6 copy.137
  320.5 3.9 all-to-all-start.4
  324.4 13.3 %pad_maximum_fusion.1 = bf16[6,8,10,128,128]{4,1,3,2,0:T(8,128)(2,1)} fusion(bf16[6,8,1,128,128]{4,1,3,2,0:T(8,128)(2,1)} %copy.137, bf16[6,8,8,128,128]{4,1,3,2,0:T(8,128)(2,1)} %get-tuple-element.241, bf16[6,8,1,128,128]{4,1,3,2,0:T(8,128)(2,1)} %copy.136), kind=kLoop, calls=%fused_computation.97 | loop fusion | flops 15728640 | bytes 31457280 | tf_op jit(solution)/shard_map/concatenate | solution.py:21
  340.5 24.7 %all_gather.7 = f32[8,128,128]{1,2,0:T(8,128)} all-gather(f32[8,128,8]{1,2,0:T(8,128)S(1)} %all_to_all.75), channel_id=1, replica_groups=mesh['space'=8,'mode'=16] {'mode'}, dimensions={2}, use_global_device_ids=true | all-gather | bytes 557056 | tf_op jit(solution)/shard_map/all_gather | solution.py:181
  367.3 136.7 %while.29 = (s32[]{:T(128)}, f32[4,8,128,128]{3,0,2,1:T(4,128)}, f32[6,8]{1,0:T(8,128)S(1)}, f32[6,8]{1,0:T(8,128)S(1)}, f32[6,8]{1,0:T(8,128)S(1)}, /*index=5*/...) while((s32[]{:T(128)}, f32[4,8,128,128]{3,0,2,1:T(4,128)}, ...), condition=%wide.region_7.8_spmd.clone, body=%wide.region_6.7_spmd.clone.sunk | while | flops 76808344 | bytes 54527136 | solution.py:206
  369.5 2.5 slice.1269
  373.2 16.9 %select_add_fusion.5 = f32[4,8,128,128]{3,0,2,1:T(4,128)} fusion(f32[4,8,128,128]{3,0,2,1:T(4,128)} %get-tuple-element.739, f32[8,8,128,128]{3,0,2,1:T(8,128)} %slice.1269, f32[8,10,128,128]{3,0,2,1:T(8,128)} %copy-done, f32[8,128,128]{2,1,0:T(8,128)} %get-tuple-element.757, f32[8]{0:T(128)S(1)} %fusion.183, f32[8]{0:T(128)S(1)} %get-tuple-element.683, ...), kind=kOutput, calls=%fused_computation.62.clone.1 | convolution fusion | flops 75497568 | bytes 17301888 | tf_op jit(solution)/shard_map/while/body/eval_jaxpr/km,mzxy->kzxy/dot_general | solution.py:100
  392.3 2.5 slice.1269
  396.0 16.9 %select_add_fusion.5 = f32[4,8,128,128]{3,0,2,1:T(4,128)} fusion(f32[4,8,128,128]{3,0,2,1:T(4,128)} %get-tuple-element.739, f32[8,8,128,128]{3,0,2,1:T(8,128)} %slice.1269, f32[8,10,128,128]{3,0,2,1:T(8,128)} %copy-done, f32[8,128,128]{2,1,0:T(8,128)} %get-tuple-element.757, f32[8]{0:T(128)S(1)} %fusion.183, f32[8]{0:T(128)S(1)} %get-tuple-element.683, ...), kind=kOutput, calls=%fused_computation.62.clone.1 | convolution fusion | flops 75497568 | bytes 17301888 | tf_op jit(solution)/shard_map/while/body/eval_jaxpr/km,mzxy->kzxy/dot_general | solution.py:100
  415.1 2.5 slice.1269
  418.8 16.9 %select_add_fusion.5 = f32[4,8,128,128]{3,0,2,1:T(4,128)} fusion(f32[4,8,128,128]{3,0,2,1:T(4,128)} %get-tuple-element.739, f32[8,8,128,128]{3,0,2,1:T(8,128)} %slice.1269, f32[8,10,128,128]{3,0,2,1:T(8,128)} %copy-done, f32[8,128,128]{2,1,0:T(8,128)} %get-tuple-element.757, f32[8]{0:T(128)S(1)} %fusion.183, f32[8]{0:T(128)S(1)} %get-tuple-element.683, ...), kind=kOutput, calls=%fused_computation.62.clone.1 | convolution fusion | flops 75497568 | bytes 17301888 | tf_op jit(solution)/shard_map/while/body/eval_jaxpr/km,mzxy->kzxy/dot_general | solution.py:100
  437.9 2.5 slice.1269
  441.5 16.9 %select_add_fusion.5 = f32[4,8,128,128]{3,0,2,1:T(4,128)} fusion(f32[4,8,128,128]{3,0,2,1:T(4,128)} %get-tuple-element.739, f32[8,8,128,128]{3,0,2,1:T(8,128)} %slice.1269, f32[8,10,128,128]{3,0,2,1:T(8,128)} %copy-done, f32[8,128,128]{2,1,0:T(8,128)} %get-tuple-element.757, f32[8]{0:T(128)S(1)} %fusion.183, f32[8]{0:T(128)S(1)} %get-tuple-element.683, ...), kind=kOutput, calls=%fused_computation.62.clone.1 | convolution fusion | flops 75497568 | bytes 17301888 | tf_op jit(solution)/shard_map/while/body/eval_jaxpr/km,mzxy->kzxy/dot_general | solution.py:100
  460.7 2.5 slice.1269
  464.3 16.9 %select_add_fusion.5 = f32[4,8,128,128]{3,0,2,1:T(4,128)} fusion(f32[4,8,128,128]{3,0,2,1:T(4,128)} %get-tuple-element.739, f32[8,8,128,128]{3,0,2,1:T(8,128)} %slice.1269, f32[8,10,128,128]{3,0,2,1:T(8,128)} %copy-done, f32[8,128,128]{2,1,0:T(8,128)} %get-tuple-element.757, f32[8]{0:T(128)S(1)} %fusion.183, f32[8]{0:T(128)S(1)} %get-tuple-element.683, ...), kind=kOutput, calls=%fused_computation.62.clone.1 | convolution fusion | flops 75497568 | bytes 17301888 | tf_op jit(solution)/shard_map/while/body/eval_jaxpr/km,mzxy->kzxy/dot_general | solution.py:100
  483.5 2.5 slice.1269
  487.1 16.9 %select_add_fusion.5 = f32[4,8,128,128]{3,0,2,1:T(4,128)} fusion(f32[4,8,128,128]{3,0,2,1:T(4,128)} %get-tuple-element.739, f32[8,8,128,128]{3,0,2,1:T(8,128)} %slice.1269, f32[8,10,128,128]{3,0,2,1:T(8,128)} %copy-done, f32[8,128,128]{2,1,0:T(8,128)} %get-tuple-element.757, f32[8]{0:T(128)S(1)} %fusion.183, f32[8]{0:T(128)S(1)} %get-tuple-element.683, ...), kind=kOutput, calls=%fused_computation.62.clone.1 | convolution fusion | flops 75497568 | bytes 17301888 | tf_op jit(solution)/shard_map/while/body/eval_jaxpr/km,mzxy->kzxy/dot_general | solution.py:100
  504.0 2.9 copy.151
  508.8 33.5 %all_to_all.88 = f32[16,4,8,128,8]{3,4,2,1,0:T(8,128)} all-to-all(f32[16,4,8,128,8]{3,4,2,1,0:T(8,128)S(1)} %copy.152), channel_id=1, replica_groups=mesh['space'=8,'mode'=16] {'mode'}, dimensions={0} | all-to-all | bytes 4194304 | tf_op jit(solution)/shard_map/all_to_all | solution.py:49
  544.0 2.9 copy.153
  546.8 2.7 reshape.256
  549.5 8.2 %all_to_all.89 = f32[8,1,4096]{2,1,0:T(1,128)S(1)} all-to-all(f32[8,1,4096]{2,1,0:T(1,128)S(1)} %reshape.256), channel_id=1, replica_groups=mesh['space'=8,'mode'=16] {'space'}, dimensions={0} | all-to-all | bytes 262144 | tf_op jit(solution)/shard_map/all_to_all | solution.py:243
  558.6 2.5 reshape.257
  561.1 3.4 copy.155
  566.8 3.5 collective-permute-start.12
  573.1 5.2 collective-permute-done.12
  579.7 4.0 collective-permute-done.13
  586.0 7.0 %collective-permute-start.14 = (bf16[3,24,4,64]{3,2,1,0:T(4,128)(2,1)S(1)}, bf16[3,24,4,64]{3,2,1,0:T(4,128)(2,1)S(1)}, u32[]{:S(2)}, u32[]{:S(2)}) collective-permute-start(bf16[3,24,4,64]{3,2,1,0:T(4,128)(2,1)S(1)} %get-tuple-element.526), channel_id=1, source_target_pairs={{0,1},{1,2},{2,3},{3,4},{4,5},{5,6},{6,7},{7,8},{8,9},{9,10},{10,1... | collective-permute-start | bytes 110600 | tf_op jit(solution)/shard_map/ppermute | solution.py:23
  599.8 2.5 collective-permute-done.15
  (242 shorter events, 127.3 us)
Async XLA Ops:
  0.6 9.4 %copy-start.4 = (f32[16,8,64]{2,1,0:T(8,128)S(1)}, f32[16,8,64]{2,1,0:T(8,128)}, u32[]{:S(2)}) copy-start(f32[16,8,64]{2,1,0:T(8,128)} %param.14) | copy-start | bytes 98308
  0.6 16.8 %copy-start.11 = (s32[48]{0:T(128)S(1)}, s32[48]{0:T(128)}, u32[]{:S(2)}) copy-start(s32[48]{0:T(128)} %param.17) | copy-start | bytes 580
  0.7 16.8 %copy-start.10 = (f32[6]{0:T(128)S(1)}, f32[6]{0:T(128)}, u32[]{:S(2)}) copy-start(f32[6]{0:T(128)} %param.19) | copy-start | bytes 76
  0.7 16.9 %copy-start.7 = (s32[48]{0:T(128)S(1)}, s32[48]{0:T(128)}, u32[]{:S(2)}) copy-start(s32[48]{0:T(128)} %param.18) | copy-start | bytes 580
  0.7 17.0 %copy-start.8 = (f32[48]{0:T(128)S(1)}, f32[48]{0:T(128)}, u32[]{:S(2)}) copy-start(f32[48]{0:T(128)} %param.15) | copy-start | bytes 580
  0.7 17.0 %copy-start.9 = (f32[48]{0:T(128)S(1)}, f32[48]{0:T(128)}, u32[]{:S(2)}) copy-start(f32[48]{0:T(128)} %param.16) | copy-start | bytes 580
  4.7 75.4 %collective-permute-start = (bf16[48,1,128,128]{3,2,1,0:T(8,128)(2,1)}, bf16[48,1,128,128]{3,2,1,0:T(8,128)(2,1)}, u32[]{:S(2)}, u32[]{:S(2)}) collective-permute-start(bf16[48,1,128,128]{3,2,1,0:T(8,128)(2,1)} %get-tuple-element.508), channel_id=1, source_target_pairs={{0,16},{16,32},{32,48},{48,64},{64,80},{80,96},{96,112},{1,17},{17... | collective-permute-start | bytes 4718600 | tf_op jit(solution)/shard_map/ppermute | solution.py:23
  8.1 71.9 %collective-permute-start.1 = (bf16[48,1,128,128]{3,2,1,0:T(8,128)(2,1)}, bf16[48,1,128,128]{3,2,1,0:T(8,128)(2,1)}, u32[]{:S(2)}, u32[]{:S(2)}) collective-permute-start(bf16[48,1,128,128]{3,2,1,0:T(8,128)(2,1)} %get-tuple-element.509), channel_id=1, source_target_pairs={{16,0},{32,16},{48,32},{64,48},{80,64},{96,80},{112,96},{17,1},{33... | collective-permute-start | bytes 4718600 | tf_op jit(solution)/shard_map/ppermute | solution.py:25
  11.0 36.7 %all-to-all-start = ((f32[8,1,1024]{2,1,0:T(1,128)}), f32[8,1,1024]{2,1,0:T(1,128)S(1)}, u32[]{:S(2)}, u32[]{:S(2)}) async-start(f32[8,1,1024]{2,1,0:T(1,128)} %reshape.250), calls=%async_computation | async-start | bytes 65536 | tf_op jit(solution)/shard_map/all_to_all | solution.py:180
  49.0 148.6 %all-to-all-start.3 = ((f32[16,1,1]{2,1,0:T(1,128)}), f32[16,1,1]{2,1,0:T(1,128)S(1)}, u32[]{:S(2)}, u32[]{:S(2)}) async-start(f32[16,1,1]{2,1,0:T(1,128)} %broadcast_in_dim.52), calls=%async_computation.3 | async-start | bytes 16384 | tf_op jit(solution)/shard_map/all_to_all | solution.py:34
  194.3 12.9 %copy-start.5 = (f32[16,8,64]{2,1,0:T(8,128)S(1)}, f32[16,8,64]{2,1,0:T(8,128)}, u32[]{:S(2)}) copy-start(f32[16,8,64]{2,1,0:T(8,128)} %param.20) | copy-start | bytes 98308
  194.3 12.9 %copy-start.6 = (s32[16,8,64]{2,1,0:T(8,128)S(1)}, s32[16,8,64]{2,1,0:T(8,128)}, u32[]{:S(2)}) copy-start(s32[16,8,64]{2,1,0:T(8,128)} %param.21) | copy-start | bytes 98308
  197.6 36.4 %all-to-all-start.1 = ((f32[16,4,8,128,8]{3,4,2,1,0:T(8,128)}), f32[16,4,8,128,8]{3,4,2,1,0:T(8,128)S(1)}, u32[]{:S(2)}, u32[]{:S(2)}) async-start(f32[16,4,8,128,8]{3,4,2,1,0:T(8,128)} %copy.139), calls=%async_computation.1 | async-start | bytes 4194304 | tf_op jit(solution)/shard_map/all_to_all | solution.py:49
  207.2 22.2 %collective-permute-start.8 = (bf16[4,8,64]{2,1,0:T(8,128)(2,1)S(1)}, bf16[4,8,64]{2,1,0:T(8,128)(2,1)S(1)}, u32[]{:S(2)}, u32[]{:S(2)}) collective-permute-start(bf16[4,8,64]{2,1,0:T(8,128)(2,1)S(1)} %get-tuple-element.532), channel_id=1, source_target_pairs={{0,16},{16,32},{32,48},{48,64},{64,80},{80,96},{96,112},{1,17},{17... | collective-permute-start | bytes 12296 | tf_op jit(solution)/shard_map/ppermute | solution.py:23
  209.1 20.3 %collective-permute-start.9 = (bf16[4,8,64]{2,1,0:T(8,128)(2,1)S(1)}, bf16[4,8,64]{2,1,0:T(8,128)(2,1)S(1)}, u32[]{:S(2)}, u32[]{:S(2)}) collective-permute-start(bf16[4,8,64]{2,1,0:T(8,128)(2,1)S(1)} %get-tuple-element.533), channel_id=1, source_target_pairs={{16,0},{32,16},{48,32},{64,48},{80,64},{96,80},{112,96},{17,1},{33... | collective-permute-start | bytes 12296 | tf_op jit(solution)/shard_map/ppermute | solution.py:25
  223.4 78.0 %collective-permute-start.2 = (bf16[48,1,128,128]{3,2,1,0:T(8,128)(2,1)}, bf16[48,1,128,128]{3,2,1,0:T(8,128)(2,1)}, u32[]{:S(2)}, u32[]{:S(2)}) collective-permute-start(bf16[48,1,128,128]{3,2,1,0:T(8,128)(2,1)} %get-tuple-element.506), channel_id=1, source_target_pairs={{0,16},{16,32},{32,48},{48,64},{64,80},{80,96},{96,112},{1,17},{17... | collective-permute-start | bytes 4718600 | tf_op jit(solution)/shard_map/ppermute | solution.py:23
  227.5 77.6 %collective-permute-start.3 = (bf16[48,1,128,128]{3,2,1,0:T(8,128)(2,1)}, bf16[48,1,128,128]{3,2,1,0:T(8,128)(2,1)}, u32[]{:S(2)}, u32[]{:S(2)}) collective-permute-start(bf16[48,1,128,128]{3,2,1,0:T(8,128)(2,1)} %get-tuple-element.507), channel_id=1, source_target_pairs={{16,0},{32,16},{48,32},{64,48},{80,64},{96,80},{112,96},{17,1},{33... | collective-permute-start | bytes 4718600 | tf_op jit(solution)/shard_map/ppermute | solution.py:25
  237.6 30.6 %all-to-all-start.2 = ((f32[8,1,4096]{2,1,0:T(1,128)}), f32[8,1,4096]{2,1,0:T(1,128)S(1)}, u32[]{:S(2)}, u32[]{:S(2)}) async-start(f32[8,1,4096]{2,1,0:T(1,128)} %reshape.252), calls=%async_computation.2 | async-start | bytes 262144 | tf_op jit(solution)/shard_map/all_to_all | solution.py:243
  241.6 33.1 %collective-permute-start.10 = (bf16[24,4,64]{2,1,0:T(4,128)(2,1)S(1)}, bf16[24,4,64]{2,1,0:T(4,128)(2,1)S(1)}, u32[]{:S(2)}, u32[]{:S(2)}) collective-permute-start(bf16[24,4,64]{2,1,0:T(4,128)(2,1)S(1)} %get-tuple-element.530), channel_id=1, source_target_pairs={{0,1},{1,2},{2,3},{3,4},{4,5},{5,6},{6,7},{7,8},{8,9},{9,10},{10,1... | collective-permute-start | bytes 36872 | tf_op jit(solution)/shard_map/ppermute | solution.py:23
  247.5 30.6 %collective-permute-start.11 = (bf16[24,4,64]{2,1,0:T(4,128)(2,1)S(1)}, bf16[24,4,64]{2,1,0:T(4,128)(2,1)S(1)}, u32[]{:S(2)}, u32[]{:S(2)}) collective-permute-start(bf16[24,4,64]{2,1,0:T(4,128)(2,1)S(1)} %get-tuple-element.531), channel_id=1, source_target_pairs={{1,0},{2,1},{3,2},{4,3},{5,4},{6,5},{7,6},{8,7},{9,8},{10,9},{11,1... | collective-permute-start | bytes 36872 | tf_op jit(solution)/shard_map/ppermute | solution.py:25
  271.5 24.8 %copy-start.2 = (f32[4,8,8,16,8]{3,4,2,1,0:T(8,128)}, f32[4,8,8,16,8]{3,4,2,1,0:T(8,128)S(1)}, u32[]{:S(2)}) copy-start(f32[4,8,8,16,8]{3,4,2,1,0:T(8,128)S(1)} %copy.142) | copy-start | bytes 393220
  272.8 10.9 %collective-permute-start.4 = (bf16[3,4,8,64]{1,2,3,0:T(8,128)(2,1)}, bf16[3,4,8,64]{1,2,3,0:T(8,128)(2,1)S(1)}, u32[]{:S(2)}, u32[]{:S(2)}) collective-permute-start(bf16[3,4,8,64]{1,2,3,0:T(8,128)(2,1)} %get-tuple-element.522), channel_id=1, source_target_pairs={{0,16},{16,32},{32,48},{48,64},{64,80},{80,96},{96,112},{1,17},{17... | collective-permute-start | bytes 36872 | tf_op jit(solution)/shard_map/ppermute | solution.py:23
  274.7 13.1 %collective-permute-start.5 = (bf16[3,4,8,64]{1,2,3,0:T(8,128)(2,1)}, bf16[3,4,8,64]{1,2,3,0:T(8,128)(2,1)}, u32[]{:S(2)}, u32[]{:S(2)}) collective-permute-start(bf16[3,4,8,64]{1,2,3,0:T(8,128)(2,1)} %get-tuple-element.523), channel_id=1, source_target_pairs={{16,0},{32,16},{48,32},{64,48},{80,64},{96,80},{112,96},{17,1},{33... | collective-permute-start | bytes 36872 | tf_op jit(solution)/shard_map/ppermute | solution.py:25
  289.3 19.4 %collective-permute-start.6 = (bf16[3,24,4,64]{3,2,1,0:T(4,128)(2,1)S(1)}, bf16[3,24,4,64]{3,2,1,0:T(4,128)(2,1)S(1)}, u32[]{:S(2)}, u32[]{:S(2)}) collective-permute-start(bf16[3,24,4,64]{3,2,1,0:T(4,128)(2,1)S(1)} %get-tuple-element.528), channel_id=1, source_target_pairs={{0,1},{1,2},{2,3},{3,4},{4,5},{5,6},{6,7},{7,8},{8,9},{9,10},{10,1... | collective-permute-start | bytes 110600 | tf_op jit(solution)/shard_map/ppermute | solution.py:23
  296.3 12.3 %collective-permute-start.7 = (bf16[3,24,4,64]{3,2,1,0:T(4,128)(2,1)S(1)}, bf16[3,24,4,64]{3,2,1,0:T(4,128)(2,1)S(1)}, u32[]{:S(2)}, u32[]{:S(2)}) collective-permute-start(bf16[3,24,4,64]{3,2,1,0:T(4,128)(2,1)S(1)} %get-tuple-element.529), channel_id=1, source_target_pairs={{1,0},{2,1},{3,2},{4,3},{5,4},{6,5},{7,6},{8,7},{9,8},{10,9},{11,1... | collective-permute-start | bytes 110600 | tf_op jit(solution)/shard_map/ppermute | solution.py:25
  311.7 1.0 copy-start.1
  320.5 17.3 %all-to-all-start.4 = ((f32[8,1,1024]{2,1,0:T(1,128)}), f32[8,1,1024]{2,1,0:T(1,128)S(1)}, u32[]{:S(2)}, u32[]{:S(2)}) async-start(f32[8,1,1024]{2,1,0:T(1,128)} %reshape.254), calls=%async_computation.4 | async-start | bytes 65536 | tf_op jit(solution)/shard_map/all_to_all | solution.py:180
  369.5 3.7 copy-start
  392.3 3.7 copy-start
  415.1 3.7 copy-start
  437.9 3.7 copy-start
  460.7 3.7 copy-start
  483.4 3.7 copy-start
  566.8 11.6 %collective-permute-start.12 = (bf16[3,4,8,64]{1,2,3,0:T(8,128)(2,1)}, bf16[3,4,8,64]{1,2,3,0:T(8,128)(2,1)}, u32[]{:S(2)}, u32[]{:S(2)}) collective-permute-start(bf16[3,4,8,64]{1,2,3,0:T(8,128)(2,1)} %get-tuple-element.524), channel_id=1, source_target_pairs={{0,16},{16,32},{32,48},{48,64},{64,80},{80,96},{96,112},{1,17},{17... | collective-permute-start | bytes 36872 | tf_op jit(solution)/shard_map/ppermute | solution.py:23
  570.3 13.3 %collective-permute-start.13 = (bf16[3,4,8,64]{1,2,3,0:T(8,128)(2,1)}, bf16[3,4,8,64]{1,2,3,0:T(8,128)(2,1)}, u32[]{:S(2)}, u32[]{:S(2)}) collective-permute-start(bf16[3,4,8,64]{1,2,3,0:T(8,128)(2,1)} %get-tuple-element.525), channel_id=1, source_target_pairs={{16,0},{32,16},{48,32},{64,48},{80,64},{96,80},{112,96},{17,1},{33... | collective-permute-start | bytes 36872 | tf_op jit(solution)/shard_map/ppermute | solution.py:25
  586.0 13.2 %collective-permute-start.14 = (bf16[3,24,4,64]{3,2,1,0:T(4,128)(2,1)S(1)}, bf16[3,24,4,64]{3,2,1,0:T(4,128)(2,1)S(1)}, u32[]{:S(2)}, u32[]{:S(2)}) collective-permute-start(bf16[3,24,4,64]{3,2,1,0:T(4,128)(2,1)S(1)} %get-tuple-element.526), channel_id=1, source_target_pairs={{0,1},{1,2},{2,3},{3,4},{4,5},{5,6},{6,7},{7,8},{8,9},{9,10},{10,1... | collective-permute-start | bytes 110600 | tf_op jit(solution)/shard_map/ppermute | solution.py:23
  592.9 9.4 %collective-permute-start.15 = (bf16[3,24,4,64]{3,2,1,0:T(4,128)(2,1)S(1)}, bf16[3,24,4,64]{3,2,1,0:T(4,128)(2,1)}, u32[]{:S(2)}, u32[]{:S(2)}) collective-permute-start(bf16[3,24,4,64]{3,2,1,0:T(4,128)(2,1)S(1)} %get-tuple-element.527), channel_id=1, source_target_pairs={{1,0},{2,1},{3,2},{4,3},{5,4},{6,5},{7,6},{8,7},{9,8},{10,9},{11,1... | collective-permute-start | bytes 110600 | tf_op jit(solution)/shard_map/ppermute | solution.py:25
  599.2 0.6 copy-start.3
where the time goes:
time: 626 us; the launch traced here: 615 us
  matrix products  143 us (23%)
  local copies, waits for them, and re-layouts  113 us (18%)
  other arithmetic  111 us (18%)
  starting transfers between devices  86.7 us (14%)
  blocking collectives  86.3 us (14%)
  waiting for transfers between devices  71.9 us (11%)
    dot_general x12, matrix products, upwind(): jnp.einsum('km,mzxy->kzxy', weights, updated, precision=lax.Precision.HIG...  143 us
    all_gather x2, blocking collectives, to_slab(): return lax.all_gather(moved, 'mode', axis=2, tiled=True)  44.6 us
    ppermute x8, starting transfers between devices, padded_2(): lax.ppermute(tail, axis, [(i, (i + 1) % count) for i in range(ends)])  34.7 us
    all_to_all x1, blocking collectives, sum_at_owner(): lax.all_to_all(in_blocks(shard, dim, length), axis, 0, 0, tiled=True)  33.5 us
    dynamic_update_slice x6, other arithmetic, kinetic(): moments, news = lax.scan(step, start, (shaped,) + params)  31.9 us
    all_to_all x2, waiting for transfers between devices, to_slab(): lax.all_to_all(upright, 'space', split_axis=0, concat_axis=1, tiled=True)  29 us
    concatenate x8, other arithmetic, padded_2(): jnp.concatenate([lax.ppermute(tail, axis, [(i, (i + 1) % count) for i in...  29 us
    convert_element_type x12, other arithmetic, step(): block.astype(jnp.float32)  23.6 us
  transfers between devices with their start and end apart: 21, of which 8 were waited for; matrix products, arithmetic and copies ran while one was open for 28% of the time, Pallas kernels for 0%

commit v1 on v0

--- a/solution.py
+++ b/solution.py
@@ -178,7 +178,9 @@
 def to_slab(block):
     upright = jnp.transpose(block, (2, 0, 1))
     moved = lax.all_to_all(upright, "space", split_axis=0, concat_axis=1, tiled=True)
-    return lax.all_gather(moved, "mode", axis=2, tiled=True)
+    return jnp.concatenate(
+        lax.all_to_all(jnp.stack([moved] * lax.axis_size("mode")), "mode", 0, 0), axis=2
+    )
 
 
 def kinetic(state, temp_slab, velocity, rates, capacity):

time: 626 us -> 693 us (1.11)
  other arithmetic: 111 us -> 163 us
  blocking collectives: 86.3 us -> 41.6 us
  local copies, waits for them, and re-layouts: 113 us -> 149 us
  waiting for transfers between devices: 71.9 us -> 83.8 us
  starting transfers between devices: 86.7 us -> 98.1 us
    dynamic_update_slice x6, other arithmetic: 31.9 us -> 84.3 us  [kinetic(): moments, news = lax.scan(step, start, (shaped,) + params)]
    all_gather x2 -> x0, blocking collectives: 44.6 us -> none  [to_slab(): return lax.all_gather(moved, 'mode', axis=2, tiled=True)]
    all_to_all x1, waiting for transfers between devices: 18.8 us -> 2.6 us  [per_device(): lax.all_to_all(reduced, 'space', split_axis=2, concat_axis=1, tiled=True)]
    all_to_all x0 -> x2, starting transfers between devices: none -> 15.4 us  [to_slab(): lax.all_to_all(jnp.stack([moved] * lax.axis_size('mode')), 'mode', 0, 0)]
    slice x12, local copies, waits for them, and re-layouts: 16.5 us -> 30.1 us  [upwind(): current = padded[:, 1:-1]]
    mul x12 -> x24, local copies, waits for them, and re-layouts: 0.09 us -> 11.5 us  [upwind(): widen(capacity) * temp_slab[None] - current]
    ppermute x8, waiting for transfers between devices: 9.12 us -> 20.5 us  [padded_2(): lax.ppermute(tail, axis, [(i, (i + 1) % count) for i in range(ends)])]
    all_to_all x0 -> x2, waiting for transfers between devices: none -> 8.88 us  [to_slab(): lax.all_to_all(jnp.stack([moved] * lax.axis_size('mode')), 'mode', 0, 0)]
  transfers between devices with their start and end apart: 21 -> 23, of which waited for: 8 -> 10; matrix products, arithmetic and copies ran while one was open for 28% -> 37% of each run, Pallas kernels for 0% -> 0%
where the time goes in v1:
time: 693 us; the launch traced here: 681 us
  other arithmetic  163 us (24%)
  local copies, waits for them, and re-layouts  149 us (22%)
  matrix products  142 us (20%)
  starting transfers between devices  98.1 us (14%)
  waiting for transfers between devices  83.8 us (12%)
  blocking collectives  41.6 us (6%)
    dot_general x12, matrix products, upwind(): jnp.einsum('km,mzxy->kzxy', weights, updated, precision=lax.Precision.HIG...  142 us
    dynamic_update_slice x6, other arithmetic, kinetic(): moments, news = lax.scan(step, start, (shaped,) + params)  84.3 us
    ppermute x8, starting transfers between devices, padded_2(): lax.ppermute(tail, axis, [(i, (i + 1) % count) for i in range(ends)])  36.8 us
    all_to_all x1, blocking collectives, sum_at_owner(): lax.all_to_all(in_blocks(shard, dim, length), axis, 0, 0, tiled=True)  34 us
    all_to_all x2, waiting for transfers between devices, to_slab(): lax.all_to_all(upright, 'space', split_axis=0, concat_axis=1, tiled=True)  30.1 us
    slice x12, local copies, waits for them, and re-layouts, upwind(): current = padded[:, 1:-1]  30.1 us
    concatenate x8, other arithmetic, padded_2(): jnp.concatenate([lax.ppermute(tail, axis, [(i, (i + 1) % count) for i in...  27.1 us
    convert_element_type x12, other arithmetic, step(): block.astype(jnp.float32)  23.6 us
  transfers between devices with their start and end apart: 23, of which 10 were waited for; matrix products, arithmetic and copies ran while one was open for 37% of the time, Pallas kernels for 0%

profile of v1, /device:TPU:31, one launch (start us, length us, event | category | flops | bytes accessed | tf_op | source)
XLA Modules:
  0.0 680.6 jit_solution(744312604416130340)
XLA Ops:
  0.7 4.0 fusion.165
  4.7 3.4 collective-permute-start
  11.0 6.4 all-to-all-start
  17.6 30.1 %all-to-all-done = f32[8,1,1024]{2,1,0:T(1,128)S(1)} async-done(((f32[8,1,1024]{2,1,0:T(1,128)}), f32[8,1,1024]{2,1,0:T(1,128)S(1)}, u32[]{:S(2)}, u32[]{:S(2)}) %all-to-all-start) | async-done | bytes 32800 | tf_op jit(solution)/shard_map/all_to_all | solution.py:180
  50.3 9.2 %all-to-all-start.1 = ((f32[16,8,128,8]{2,3,1,0:T(8,128)}), f32[16,8,128,8]{2,3,1,0:T(8,128)S(1)}, u32[]{:S(2)}, u32[]{:S(2)}) async-start(f32[16,8,128,8]{2,3,1,0:T(8,128)} %stack.19), calls=%async_computation.1 | async-start | bytes 1048576 | tf_op jit(solution)/shard_map/all_to_all | solution.py:182
  60.6 8.9 %all-to-all-done.1 = f32[16,8,128,8]{2,3,1,0:T(8,128)S(1)} async-done(((f32[16,8,128,8]{2,3,1,0:T(8,128)}), f32[16,8,128,8]{2,3,1,0:T(8,128)S(1)}, u32[]{:S(2)}, u32[]{:S(2)}) %all-to-all-start.1) | async-done | bytes 524320 | tf_op jit(solution)/shard_map/all_to_all | solution.py:182
  70.8 5.7 all-to-all-start.4
  76.5 13.3 %pad_maximum_fusion = bf16[48,10,128,128]{3,2,1,0:T(8,128)(2,1)} fusion(bf16[48,1,128,128]{3,2,1,0:T(8,128)(2,1)} %collective-permute-done.1, bf16[48,8,128,128]{3,2,1,0:T(8,128)(2,1)} %param.13, bf16[48,1,128,128]{3,2,1,0:T(8,128)(2,1)} %collective-permute-done), kind=kLoop, calls=%fused_computation.96 | loop fusion | flops 15728640 | bytes 31457280 | tf_op jit(solution)/shard_map/concatenate | solution.py:21
  89.8 172.2 %while.28 = (s32[]{:T(128)}, f32[4,8,128,128]{3,0,2,1:T(4,128)S(1)}, bf16[6,8,8,128,128]{4,1,3,2,0:T(8,128)(2,1)}, f32[6,8]{1,0:T(8,128)S(1)}, f32[6,8]{1,0:T(8,...) while((s32[]{:T(128)}, ...), condition=%wide.region_2.3_spmd.clone, body=%wide.region_1.2_spmd.clone.sunk | while | flops 77856920 | bytes 71304872 | solution.py:208
  93.6 2.5 slice.1262
  97.5 14.0 %bitcast_dynamic-update-slice_fusion.2 = (bf16[6,8,8,128,128]{4,1,3,2,0:T(8,128)(2,1)}, f32[8,8,128,128]{3,0,2,1:T(8,128)}) fusion(bf16[6,8,8,128,128]{4,1,3,2,0:T(8,128)(2,1)} %get-tuple-element.696, s32[]{:T(128)} %get-tuple-element.694, f32[8,8,128,128]{3,0,2,1:T(8,128)} %slice.1262, f32[8,128,128]{2,1,0:T(8,128)S(1)} %copy.187, ...), kind=kLoop, calls=%fused_computation.19.clone.1 | loop fusion | flops 25165824 | bytes 19399424 | tf_op jit(solution)/shard_map/while/body/jit(dynamic_update_index_in_dim)/dynamic_update_slice | solution.py:208
  111.5 7.0 %select_add_fusion.4 = f32[4,8,128,128]{3,0,2,1:T(4,128)S(1)} fusion(f32[4,8,128,128]{3,0,2,1:T(4,128)S(1)} %get-tuple-element.695, f32[8,8,128,128]{3,0,2,1:T(8,128)} %get-tuple-element.662, pred[]{:T(512)S(6)} %compare.22, f32[1,8]{1,0:T(1,128)S(1)} %get-tuple-element.656, f32[1,8]{1,0:T(1,128)S(1)} %get-tuple-element.658, ...), kind=kOutput, calls=%fused_computation.20.clone.1 | convolution fusion | flops 51380320 | bytes 8388737 | tf_op jit(solution)/shard_map/while/body/eval_jaxpr/km,mzxy->kzxy/dot_general | solution.py:100
  126.2 14.0 %bitcast_dynamic-update-slice_fusion.2 = (bf16[6,8,8,128,128]{4,1,3,2,0:T(8,128)(2,1)}, f32[8,8,128,128]{3,0,2,1:T(8,128)}) fusion(bf16[6,8,8,128,128]{4,1,3,2,0:T(8,128)(2,1)} %get-tuple-element.696, s32[]{:T(128)} %get-tuple-element.694, f32[8,8,128,128]{3,0,2,1:T(8,128)} %slice.1262, f32[8,128,128]{2,1,0:T(8,128)S(1)} %copy.187, ...), kind=kLoop, calls=%fused_computation.19.clone.1 | loop fusion | flops 25165824 | bytes 19399424 | tf_op jit(solution)/shard_map/while/body/jit(dynamic_update_index_in_dim)/dynamic_update_slice | solution.py:208
  140.2 7.0 %select_add_fusion.4 = f32[4,8,128,128]{3,0,2,1:T(4,128)S(1)} fusion(f32[4,8,128,128]{3,0,2,1:T(4,128)S(1)} %get-tuple-element.695, f32[8,8,128,128]{3,0,2,1:T(8,128)} %get-tuple-element.662, pred[]{:T(512)S(6)} %compare.22, f32[1,8]{1,0:T(1,128)S(1)} %get-tuple-element.656, f32[1,8]{1,0:T(1,128)S(1)} %get-tuple-element.658, ...), kind=kOutput, calls=%fused_computation.20.clone.1 | convolution fusion | flops 51380320 | bytes 8388737 | tf_op jit(solution)/shard_map/while/body/eval_jaxpr/km,mzxy->kzxy/dot_general | solution.py:100
  151.0 2.5 slice.1262
  154.9 14.1 %bitcast_dynamic-update-slice_fusion.2 = (bf16[6,8,8,128,128]{4,1,3,2,0:T(8,128)(2,1)}, f32[8,8,128,128]{3,0,2,1:T(8,128)}) fusion(bf16[6,8,8,128,128]{4,1,3,2,0:T(8,128)(2,1)} %get-tuple-element.696, s32[]{:T(128)} %get-tuple-element.694, f32[8,8,128,128]{3,0,2,1:T(8,128)} %slice.1262, f32[8,128,128]{2,1,0:T(8,128)S(1)} %copy.187, ...), kind=kLoop, calls=%fused_computation.19.clone.1 | loop fusion | flops 25165824 | bytes 19399424 | tf_op jit(solution)/shard_map/while/body/jit(dynamic_update_index_in_dim)/dynamic_update_slice | solution.py:208
  168.9 7.0 %select_add_fusion.4 = f32[4,8,128,128]{3,0,2,1:T(4,128)S(1)} fusion(f32[4,8,128,128]{3,0,2,1:T(4,128)S(1)} %get-tuple-element.695, f32[8,8,128,128]{3,0,2,1:T(8,128)} %get-tuple-element.662, pred[]{:T(512)S(6)} %compare.22, f32[1,8]{1,0:T(1,128)S(1)} %get-tuple-element.656, f32[1,8]{1,0:T(1,128)S(1)} %get-tuple-element.658, ...), kind=kOutput, calls=%fused_computation.20.clone.1 | convolution fusion | flops 51380320 | bytes 8388737 | tf_op jit(solution)/shard_map/while/body/eval_jaxpr/km,mzxy->kzxy/dot_general | solution.py:100
  179.7 2.5 slice.1262
  183.6 14.0 %bitcast_dynamic-update-slice_fusion.2 = (bf16[6,8,8,128,128]{4,1,3,2,0:T(8,128)(2,1)}, f32[8,8,128,128]{3,0,2,1:T(8,128)}) fusion(bf16[6,8,8,128,128]{4,1,3,2,0:T(8,128)(2,1)} %get-tuple-element.696, s32[]{:T(128)} %get-tuple-element.694, f32[8,8,128,128]{3,0,2,1:T(8,128)} %slice.1262, f32[8,128,128]{2,1,0:T(8,128)S(1)} %copy.187, ...), kind=kLoop, calls=%fused_computation.19.clone.1 | loop fusion | flops 25165824 | bytes 19399424 | tf_op jit(solution)/shard_map/while/body/jit(dynamic_update_index_in_dim)/dynamic_update_slice | solution.py:208
  197.6 7.0 %select_add_fusion.4 = f32[4,8,128,128]{3,0,2,1:T(4,128)S(1)} fusion(f32[4,8,128,128]{3,0,2,1:T(4,128)S(1)} %get-tuple-element.695, f32[8,8,128,128]{3,0,2,1:T(8,128)} %get-tuple-element.662, pred[]{:T(512)S(6)} %compare.22, f32[1,8]{1,0:T(1,128)S(1)} %get-tuple-element.656, f32[1,8]{1,0:T(1,128)S(1)} %get-tuple-element.658, ...), kind=kOutput, calls=%fused_computation.20.clone.1 | convolution fusion | flops 51380320 | bytes 8388737 | tf_op jit(solution)/shard_map/while/body/eval_jaxpr/km,mzxy->kzxy/dot_general | solution.py:100
  208.4 2.5 slice.1262
  212.3 14.0 %bitcast_dynamic-update-slice_fusion.2 = (bf16[6,8,8,128,128]{4,1,3,2,0:T(8,128)(2,1)}, f32[8,8,128,128]{3,0,2,1:T(8,128)}) fusion(bf16[6,8,8,128,128]{4,1,3,2,0:T(8,128)(2,1)} %get-tuple-element.696, s32[]{:T(128)} %get-tuple-element.694, f32[8,8,128,128]{3,0,2,1:T(8,128)} %slice.1262, f32[8,128,128]{2,1,0:T(8,128)S(1)} %copy.187, ...), kind=kLoop, calls=%fused_computation.19.clone.1 | loop fusion | flops 25165824 | bytes 19399424 | tf_op jit(solution)/shard_map/while/body/jit(dynamic_update_index_in_dim)/dynamic_update_slice | solution.py:208
  226.3 7.0 %select_add_fusion.4 = f32[4,8,128,128]{3,0,2,1:T(4,128)S(1)} fusion(f32[4,8,128,128]{3,0,2,1:T(4,128)S(1)} %get-tuple-element.695, f32[8,8,128,128]{3,0,2,1:T(8,128)} %get-tuple-element.662, pred[]{:T(512)S(6)} %compare.22, f32[1,8]{1,0:T(1,128)S(1)} %get-tuple-element.656, f32[1,8]{1,0:T(1,128)S(1)} %get-tuple-element.658, ...), kind=kOutput, calls=%fused_computation.20.clone.1 | convolution fusion | flops 51380320 | bytes 8388737 | tf_op jit(solution)/shard_map/while/body/eval_jaxpr/km,mzxy->kzxy/dot_general | solution.py:100
  241.0 14.1 %bitcast_dynamic-update-slice_fusion.2 = (bf16[6,8,8,128,128]{4,1,3,2,0:T(8,128)(2,1)}, f32[8,8,128,128]{3,0,2,1:T(8,128)}) fusion(bf16[6,8,8,128,128]{4,1,3,2,0:T(8,128)(2,1)} %get-tuple-element.696, s32[]{:T(128)} %get-tuple-element.694, f32[8,8,128,128]{3,0,2,1:T(8,128)} %slice.1262, f32[8,128,128]{2,1,0:T(8,128)S(1)} %copy.187, ...), kind=kLoop, calls=%fused_computation.19.clone.1 | loop fusion | flops 25165824 | bytes 19399424 | tf_op jit(solution)/shard_map/while/body/jit(dynamic_update_index_in_dim)/dynamic_update_slice | solution.py:208
  255.1 7.0 %select_add_fusion.4 = f32[4,8,128,128]{3,0,2,1:T(4,128)S(1)} fusion(f32[4,8,128,128]{3,0,2,1:T(4,128)S(1)} %get-tuple-element.695, f32[8,8,128,128]{3,0,2,1:T(8,128)} %get-tuple-element.662, pred[]{:T(512)S(6)} %compare.22, f32[1,8]{1,0:T(1,128)S(1)} %get-tuple-element.656, f32[1,8]{1,0:T(1,128)S(1)} %get-tuple-element.658, ...), kind=kOutput, calls=%fused_computation.20.clone.1 | convolution fusion | flops 51380320 | bytes 8388737 | tf_op jit(solution)/shard_map/while/body/eval_jaxpr/km,mzxy->kzxy/dot_general | solution.py:100
  263.9 3.3 copy.149
  267.2 7.3 %all-to-all-start.2 = ((f32[16,4,8,128,8]{3,4,2,1,0:T(8,128)}), f32[16,4,8,128,8]{3,4,2,1,0:T(8,128)S(1)}, u32[]{:S(2)}, u32[]{:S(2)}) async-start(f32[16,4,8,128,8]{3,4,2,1,0:T(8,128)} %copy.149), calls=%async_computation.2 | async-start | bytes 4194304 | tf_op jit(solution)/shard_map/all_to_all | solution.py:49
  276.4 3.4 collective-permute-start.9
  279.8 3.8 collective-permute-done.9
  283.7 5.8 collective-permute-start.10
  293.0 8.2 %all-to-all-done.2 = f32[16,4,8,128,8]{3,4,2,1,0:T(8,128)S(1)} async-done(((f32[16,4,8,128,8]{3,4,2,1,0:T(8,128)}), f32[16,4,8,128,8]{3,4,2,1,0:T(8,128)S(1)}, u32[]{:S(2)}, u32[]{:S(2)}) %all-to-all-start.2) | async-done | bytes 2097184 | tf_op jit(solution)/shard_map/all_to_all | solution.py:49
  304.9 3.9 all-to-all-start.3
  310.3 2.6 all-to-all-done.3
  319.5 3.4 collective-permute-start.4
  324.8 3.1 compare_select_fusion.2
  327.9 11.5 %copy.145 = bf16[6,8,8,128,128]{4,3,2,1,0:T(8,128)(2,1)} copy(bf16[6,8,8,128,128]{4,1,3,2,0:T(8,128)(2,1)} %get-tuple-element.241) | data formatting | bytes 25165824 | tf_op jit(solution)/shard_map/while | solution.py:208
  341.5 7.3 %collective-permute-start.6 = (bf16[3,24,4,64]{3,2,1,0:T(4,128)(2,1)S(1)}, bf16[3,24,4,64]{3,2,1,0:T(4,128)(2,1)S(1)}, u32[]{:S(2)}, u32[]{:S(2)}) collective-permute-start(bf16[3,24,4,64]{3,2,1,0:T(4,128)(2,1)S(1)} %get-tuple-element.519), channel_id=1, source_target_pairs={{0,1},{1,2},{2,3},{3,4},{4,5},{5,6},{6,7},{7,8},{8,9},{9,10},{10,1... | collective-permute-start | bytes 110600 | tf_op jit(solution)/shard_map/ppermute | solution.py:23
  350.7 4.0 fusion.164
  354.7 5.1 collective-permute-start.2
  373.9 5.1 all-to-all-start.5
  379.0 14.6 %collective-permute-done.2 = bf16[48,1,128,128]{3,2,1,0:T(8,128)(2,1)} collective-permute-done((bf16[48,1,128,128]{3,2,1,0:T(8,128)(2,1)}, bf16[48,1,128,128]{3,2,1,0:T(8,128)(2,1)}, u32[]{:S(2)}, u32[]{:S(2)}) %collective-permute-start.2) | collective-permute-done | bytes 1572896 | tf_op jit(solution)/shard_map/ppermute | solution.py:23
  393.7 3.6 copy.146
  397.2 2.7 collective-permute-done.3
  400.0 3.6 copy.147
  405.6 6.2 all-to-all-start.6
  411.8 13.3 %pad_maximum_fusion.1 = bf16[6,8,10,128,128]{4,1,3,2,0:T(8,128)(2,1)} fusion(bf16[6,8,1,128,128]{4,1,3,2,0:T(8,128)(2,1)} %copy.147, bf16[6,8,8,128,128]{4,1,3,2,0:T(8,128)(2,1)} %get-tuple-element.241, bf16[6,8,1,128,128]{4,1,3,2,0:T(8,128)(2,1)} %copy.146), kind=kLoop, calls=%fused_computation.97 | loop fusion | flops 15728640 | bytes 31457280 | tf_op jit(solution)/shard_map/concatenate | solution.py:21
  427.0 145.8 %while.29 = (s32[]{:T(128)}, f32[4,8,128,128]{3,0,2,1:T(4,128)}, f32[6,8]{1,0:T(8,128)S(1)}, f32[6,8]{1,0:T(8,128)S(1)}, f32[6,8]{1,0:T(8,128)S(1)}, /*index=5*/...) while((s32[]{:T(128)}, f32[4,8,128,128]{3,0,2,1:T(4,128)}, ...), condition=%wide.region_7.8_spmd.clone, body=%wide.region_6.7_spmd.clone.sunk | while | flops 76808344 | bytes 55575712 | solution.py:208
  434.6 16.7 %select_add_fusion.5 = f32[4,8,128,128]{3,0,2,1:T(4,128)} fusion(f32[4,8,128,128]{3,0,2,1:T(4,128)} %get-tuple-element.730, f32[8,8,128,128]{3,0,2,1:T(8,128)} %slice.1269, f32[8,10,128,128]{3,0,2,1:T(8,128)} %copy-done.1, f32[8,128,128]{2,1,0:T(8,128)} %copy.188, f32[8]{0:T(128)S(1)} %fusion.183, f32[8]{0:T(128)S(1)} %get-tuple-element.674, ...), kind=kOutput, calls=%fused_computation.62.clone.1 | convolution fusion | flops 75497568 | bytes 17301888 | tf_op jit(solution)/shard_map/while/body/eval_jaxpr/km,mzxy->kzxy/dot_general | solution.py:100
  458.9 16.7 %select_add_fusion.5 = f32[4,8,128,128]{3,0,2,1:T(4,128)} fusion(f32[4,8,128,128]{3,0,2,1:T(4,128)} %get-tuple-element.730, f32[8,8,128,128]{3,0,2,1:T(8,128)} %slice.1269, f32[8,10,128,128]{3,0,2,1:T(8,128)} %copy-done.1, f32[8,128,128]{2,1,0:T(8,128)} %copy.188, f32[8]{0:T(128)S(1)} %fusion.183, f32[8]{0:T(128)S(1)} %get-tuple-element.674, ...), kind=kOutput, calls=%fused_computation.62.clone.1 | convolution fusion | flops 75497568 | bytes 17301888 | tf_op jit(solution)/shard_map/while/body/eval_jaxpr/km,mzxy->kzxy/dot_general | solution.py:100
  483.2 16.7 %select_add_fusion.5 = f32[4,8,128,128]{3,0,2,1:T(4,128)} fusion(f32[4,8,128,128]{3,0,2,1:T(4,128)} %get-tuple-element.730, f32[8,8,128,128]{3,0,2,1:T(8,128)} %slice.1269, f32[8,10,128,128]{3,0,2,1:T(8,128)} %copy-done.1, f32[8,128,128]{2,1,0:T(8,128)} %copy.188, f32[8]{0:T(128)S(1)} %fusion.183, f32[8]{0:T(128)S(1)} %get-tuple-element.674, ...), kind=kOutput, calls=%fused_computation.62.clone.1 | convolution fusion | flops 75497568 | bytes 17301888 | tf_op jit(solution)/shard_map/while/body/eval_jaxpr/km,mzxy->kzxy/dot_general | solution.py:100
  507.5 16.7 %select_add_fusion.5 = f32[4,8,128,128]{3,0,2,1:T(4,128)} fusion(f32[4,8,128,128]{3,0,2,1:T(4,128)} %get-tuple-element.730, f32[8,8,128,128]{3,0,2,1:T(8,128)} %slice.1269, f32[8,10,128,128]{3,0,2,1:T(8,128)} %copy-done.1, f32[8,128,128]{2,1,0:T(8,128)} %copy.188, f32[8]{0:T(128)S(1)} %fusion.183, f32[8]{0:T(128)S(1)} %get-tuple-element.674, ...), kind=kOutput, calls=%fused_computation.62.clone.1 | convolution fusion | flops 75497568 | bytes 17301888 | tf_op jit(solution)/shard_map/while/body/eval_jaxpr/km,mzxy->kzxy/dot_general | solution.py:100
  531.8 16.7 %select_add_fusion.5 = f32[4,8,128,128]{3,0,2,1:T(4,128)} fusion(f32[4,8,128,128]{3,0,2,1:T(4,128)} %get-tuple-element.730, f32[8,8,128,128]{3,0,2,1:T(8,128)} %slice.1269, f32[8,10,128,128]{3,0,2,1:T(8,128)} %copy-done.1, f32[8,128,128]{2,1,0:T(8,128)} %copy.188, f32[8]{0:T(128)S(1)} %fusion.183, f32[8]{0:T(128)S(1)} %get-tuple-element.674, ...), kind=kOutput, calls=%fused_computation.62.clone.1 | convolution fusion | flops 75497568 | bytes 17301888 | tf_op jit(solution)/shard_map/while/body/eval_jaxpr/km,mzxy->kzxy/dot_general | solution.py:100
  556.1 16.7 %select_add_fusion.5 = f32[4,8,128,128]{3,0,2,1:T(4,128)} fusion(f32[4,8,128,128]{3,0,2,1:T(4,128)} %get-tuple-element.730, f32[8,8,128,128]{3,0,2,1:T(8,128)} %slice.1269, f32[8,10,128,128]{3,0,2,1:T(8,128)} %copy-done.1, f32[8,128,128]{2,1,0:T(8,128)} %copy.188, f32[8]{0:T(128)S(1)} %fusion.183, f32[8]{0:T(128)S(1)} %get-tuple-element.674, ...), kind=kOutput, calls=%fused_computation.62.clone.1 | convolution fusion | flops 75497568 | bytes 17301888 | tf_op jit(solution)/shard_map/while/body/eval_jaxpr/km,mzxy->kzxy/dot_general | solution.py:100
  572.8 2.9 copy.161
  577.6 34.0 %all_to_all.92 = f32[16,4,8,128,8]{3,4,2,1,0:T(8,128)} all-to-all(f32[16,4,8,128,8]{3,4,2,1,0:T(8,128)S(1)} %copy.162), channel_id=1, replica_groups=mesh['space'=8,'mode'=16] {'mode'}, dimensions={0} | all-to-all | bytes 4194304 | tf_op jit(solution)/shard_map/all_to_all | solution.py:49
  613.3 2.8 copy.163
  616.1 2.7 reshape.270
  618.8 7.6 %all_to_all.93 = f32[8,1,4096]{2,1,0:T(1,128)S(1)} all-to-all(f32[8,1,4096]{2,1,0:T(1,128)S(1)} %reshape.270), channel_id=1, replica_groups=mesh['space'=8,'mode'=16] {'space'}, dimensions={0} | all-to-all | bytes 262144 | tf_op jit(solution)/shard_map/all_to_all | solution.py:245
  629.9 3.4 copy.165
  635.5 3.5 collective-permute-start.12
  641.3 5.8 collective-permute-done.12
  648.4 3.9 collective-permute-done.13
  652.7 6.4 collective-permute-start.14
  665.3 3.0 collective-permute-done.15
  (272 shorter events, 162.1 us)
Async XLA Ops:
  0.6 9.4 %copy-start.5 = (f32[16,8,64]{2,1,0:T(8,128)S(1)}, f32[16,8,64]{2,1,0:T(8,128)}, u32[]{:S(2)}) copy-start(f32[16,8,64]{2,1,0:T(8,128)} %param.14) | copy-start | bytes 98308
  0.6 16.8 %copy-start.13 = (s32[48]{0:T(128)S(1)}, s32[48]{0:T(128)}, u32[]{:S(2)}) copy-start(s32[48]{0:T(128)} %param.17) | copy-start | bytes 580
  0.7 16.8 %copy-start.12 = (f32[6]{0:T(128)S(1)}, f32[6]{0:T(128)}, u32[]{:S(2)}) copy-start(f32[6]{0:T(128)} %param.19) | copy-start | bytes 76
  0.7 16.9 %copy-start.9 = (s32[48]{0:T(128)S(1)}, s32[48]{0:T(128)}, u32[]{:S(2)}) copy-start(s32[48]{0:T(128)} %param.18) | copy-start | bytes 580
  0.7 59.2 %copy-start.10 = (f32[48]{0:T(128)S(1)}, f32[48]{0:T(128)}, u32[]{:S(2)}) copy-start(f32[48]{0:T(128)} %param.15) | copy-start | bytes 580
  0.7 59.2 %copy-start.11 = (f32[48]{0:T(128)S(1)}, f32[48]{0:T(128)}, u32[]{:S(2)}) copy-start(f32[48]{0:T(128)} %param.16) | copy-start | bytes 580
  4.7 71.8 %collective-permute-start = (bf16[48,1,128,128]{3,2,1,0:T(8,128)(2,1)}, bf16[48,1,128,128]{3,2,1,0:T(8,128)(2,1)}, u32[]{:S(2)}, u32[]{:S(2)}) collective-permute-start(bf16[48,1,128,128]{3,2,1,0:T(8,128)(2,1)} %get-tuple-element.499), channel_id=1, source_target_pairs={{0,16},{16,32},{32,48},{48,64},{64,80},{80,96},{96,112},{1,17},{17... | collective-permute-start | bytes 4718600 | tf_op jit(solution)/shard_map/ppermute | solution.py:23
  8.1 68.4 %collective-permute-start.1 = (bf16[48,1,128,128]{3,2,1,0:T(8,128)(2,1)}, bf16[48,1,128,128]{3,2,1,0:T(8,128)(2,1)}, u32[]{:S(2)}, u32[]{:S(2)}) collective-permute-start(bf16[48,1,128,128]{3,2,1,0:T(8,128)(2,1)} %get-tuple-element.500), channel_id=1, source_target_pairs={{16,0},{32,16},{48,32},{64,48},{80,64},{96,80},{112,96},{17,1},{33... | collective-permute-start | bytes 4718600 | tf_op jit(solution)/shard_map/ppermute | solution.py:25
  11.0 36.7 %all-to-all-start = ((f32[8,1,1024]{2,1,0:T(1,128)}), f32[8,1,1024]{2,1,0:T(1,128)S(1)}, u32[]{:S(2)}, u32[]{:S(2)}) async-start(f32[8,1,1024]{2,1,0:T(1,128)} %reshape.264), calls=%async_computation | async-start | bytes 65536 | tf_op jit(solution)/shard_map/all_to_all | solution.py:180
  50.3 19.2 %all-to-all-start.1 = ((f32[16,8,128,8]{2,3,1,0:T(8,128)}), f32[16,8,128,8]{2,3,1,0:T(8,128)S(1)}, u32[]{:S(2)}, u32[]{:S(2)}) async-start(f32[16,8,128,8]{2,3,1,0:T(8,128)} %stack.19), calls=%async_computation.1 | async-start | bytes 1048576 | tf_op jit(solution)/shard_map/all_to_all | solution.py:182
  70.8 196.4 %all-to-all-start.4 = ((f32[16,1,1]{2,1,0:T(1,128)}), f32[16,1,1]{2,1,0:T(1,128)S(1)}, u32[]{:S(2)}, u32[]{:S(2)}) async-start(f32[16,1,1]{2,1,0:T(1,128)} %broadcast_in_dim.50), calls=%async_computation.4 | async-start | bytes 16384 | tf_op jit(solution)/shard_map/all_to_all | solution.py:34
  93.6 3.7 copy-start
  122.3 3.7 copy-start
  151.0 3.7 copy-start
  179.7 3.7 copy-start
  208.4 3.7 copy-start
  237.1 3.7 copy-start
  262.0 5.2 copy-start.8
  263.9 10.5 %copy-start.6 = (f32[16,8,64]{2,1,0:T(8,128)S(1)}, f32[16,8,64]{2,1,0:T(8,128)}, u32[]{:S(2)}) copy-start(f32[16,8,64]{2,1,0:T(8,128)} %param.20) | copy-start | bytes 98308
  263.9 10.5 %copy-start.7 = (s32[16,8,64]{2,1,0:T(8,128)S(1)}, s32[16,8,64]{2,1,0:T(8,128)}, u32[]{:S(2)}) copy-start(s32[16,8,64]{2,1,0:T(8,128)} %param.21) | copy-start | bytes 98308
  267.2 34.1 %all-to-all-start.2 = ((f32[16,4,8,128,8]{3,4,2,1,0:T(8,128)}), f32[16,4,8,128,8]{3,4,2,1,0:T(8,128)S(1)}, u32[]{:S(2)}, u32[]{:S(2)}) async-start(f32[16,4,8,128,8]{3,4,2,1,0:T(8,128)} %copy.149), calls=%async_computation.2 | async-start | bytes 4194304 | tf_op jit(solution)/shard_map/all_to_all | solution.py:49
  274.5 5.3 collective-permute-start.8
  276.4 7.2 %collective-permute-start.9 = (bf16[4,8,64]{2,1,0:T(8,128)(2,1)S(1)}, bf16[4,8,64]{2,1,0:T(8,128)(2,1)S(1)}, u32[]{:S(2)}, u32[]{:S(2)}) collective-permute-start(bf16[4,8,64]{2,1,0:T(8,128)(2,1)S(1)} %get-tuple-element.524), channel_id=1, source_target_pairs={{16,0},{32,16},{48,32},{64,48},{80,64},{96,80},{112,96},{17,1},{33... | collective-permute-start | bytes 12296 | tf_op jit(solution)/shard_map/ppermute | solution.py:25
  283.7 25.2 %collective-permute-start.10 = (bf16[24,4,64]{2,1,0:T(4,128)(2,1)S(1)}, bf16[24,4,64]{2,1,0:T(4,128)(2,1)S(1)}, u32[]{:S(2)}, u32[]{:S(2)}) collective-permute-start(bf16[24,4,64]{2,1,0:T(4,128)(2,1)S(1)} %get-tuple-element.521), channel_id=1, source_target_pairs={{0,1},{1,2},{2,3},{3,4},{4,5},{5,6},{6,7},{7,8},{8,9},{9,10},{10,1... | collective-permute-start | bytes 36872 | tf_op jit(solution)/shard_map/ppermute | solution.py:23
  289.5 19.4 %collective-permute-start.11 = (bf16[24,4,64]{2,1,0:T(4,128)(2,1)S(1)}, bf16[24,4,64]{2,1,0:T(4,128)(2,1)S(1)}, u32[]{:S(2)}, u32[]{:S(2)}) collective-permute-start(bf16[24,4,64]{2,1,0:T(4,128)(2,1)S(1)} %get-tuple-element.522), channel_id=1, source_target_pairs={{1,0},{2,1},{3,2},{4,3},{5,4},{6,5},{7,6},{8,7},{9,8},{10,9},{11,1... | collective-permute-start | bytes 36872 | tf_op jit(solution)/shard_map/ppermute | solution.py:25
  304.9 7.9 %all-to-all-start.3 = ((f32[8,1,4096]{2,1,0:T(1,128)}), f32[8,1,4096]{2,1,0:T(1,128)S(1)}, u32[]{:S(2)}, u32[]{:S(2)}) async-start(f32[8,1,4096]{2,1,0:T(1,128)} %reshape.266), calls=%async_computation.3 | async-start | bytes 262144 | tf_op jit(solution)/shard_map/all_to_all | solution.py:245
  319.5 20.3 %collective-permute-start.4 = (bf16[3,4,8,64]{1,2,3,0:T(8,128)(2,1)}, bf16[3,4,8,64]{1,2,3,0:T(8,128)(2,1)}, u32[]{:S(2)}, u32[]{:S(2)}) collective-permute-start(bf16[3,4,8,64]{1,2,3,0:T(8,128)(2,1)} %get-tuple-element.513), channel_id=1, source_target_pairs={{0,16},{16,32},{32,48},{48,64},{64,80},{80,96},{96,112},{1,17},{17... | collective-permute-start | bytes 36872 | tf_op jit(solution)/shard_map/ppermute | solution.py:23
  322.9 18.2 %collective-permute-start.5 = (bf16[3,4,8,64]{1,2,3,0:T(8,128)(2,1)}, bf16[3,4,8,64]{1,2,3,0:T(8,128)(2,1)S(1)}, u32[]{:S(2)}, u32[]{:S(2)}) collective-permute-start(bf16[3,4,8,64]{1,2,3,0:T(8,128)(2,1)} %get-tuple-element.514), channel_id=1, source_target_pairs={{16,0},{32,16},{48,32},{64,48},{80,64},{96,80},{112,96},{17,1},{33... | collective-permute-start | bytes 36872 | tf_op jit(solution)/shard_map/ppermute | solution.py:25
  341.5 20.4 %collective-permute-start.6 = (bf16[3,24,4,64]{3,2,1,0:T(4,128)(2,1)S(1)}, bf16[3,24,4,64]{3,2,1,0:T(4,128)(2,1)S(1)}, u32[]{:S(2)}, u32[]{:S(2)}) collective-permute-start(bf16[3,24,4,64]{3,2,1,0:T(4,128)(2,1)S(1)} %get-tuple-element.519), channel_id=1, source_target_pairs={{0,1},{1,2},{2,3},{3,4},{4,5},{5,6},{6,7},{7,8},{8,9},{9,10},{10,1... | collective-permute-start | bytes 110600 | tf_op jit(solution)/shard_map/ppermute | solution.py:23
  348.8 13.1 %collective-permute-start.7 = (bf16[3,24,4,64]{3,2,1,0:T(4,128)(2,1)S(1)}, bf16[3,24,4,64]{3,2,1,0:T(4,128)(2,1)S(1)}, u32[]{:S(2)}, u32[]{:S(2)}) collective-permute-start(bf16[3,24,4,64]{3,2,1,0:T(4,128)(2,1)S(1)} %get-tuple-element.520), channel_id=1, source_target_pairs={{1,0},{2,1},{3,2},{4,3},{5,4},{6,5},{7,6},{8,7},{9,8},{10,9},{11,1... | collective-permute-start | bytes 110600 | tf_op jit(solution)/shard_map/ppermute | solution.py:25
  354.7 39.0 %collective-permute-start.2 = (bf16[48,1,128,128]{3,2,1,0:T(8,128)(2,1)}, bf16[48,1,128,128]{3,2,1,0:T(8,128)(2,1)}, u32[]{:S(2)}, u32[]{:S(2)}) collective-permute-start(bf16[48,1,128,128]{3,2,1,0:T(8,128)(2,1)} %get-tuple-element.497), channel_id=1, source_target_pairs={{0,16},{16,32},{32,48},{48,64},{64,80},{80,96},{96,112},{1,17},{17... | collective-permute-start | bytes 4718600 | tf_op jit(solution)/shard_map/ppermute | solution.py:23
  359.8 40.2 %collective-permute-start.3 = (bf16[48,1,128,128]{3,2,1,0:T(8,128)(2,1)}, bf16[48,1,128,128]{3,2,1,0:T(8,128)(2,1)}, u32[]{:S(2)}, u32[]{:S(2)}) collective-permute-start(bf16[48,1,128,128]{3,2,1,0:T(8,128)(2,1)} %get-tuple-element.498), channel_id=1, source_target_pairs={{16,0},{32,16},{48,32},{64,48},{80,64},{96,80},{112,96},{17,1},{33... | collective-permute-start | bytes 4718600 | tf_op jit(solution)/shard_map/ppermute | solution.py:25
  365.0 1.0 copy-start.2
  373.9 29.7 %all-to-all-start.5 = ((f32[8,1,1024]{2,1,0:T(1,128)}), f32[8,1,1024]{2,1,0:T(1,128)S(1)}, u32[]{:S(2)}, u32[]{:S(2)}) async-start(f32[8,1,1024]{2,1,0:T(1,128)} %reshape.268), calls=%async_computation.5 | async-start | bytes 65536 | tf_op jit(solution)/shard_map/all_to_all | solution.py:180
  405.6 19.5 %all-to-all-start.6 = ((f32[16,8,128,8]{2,3,1,0:T(8,128)}), f32[16,8,128,8]{2,3,1,0:T(8,128)S(1)}, u32[]{:S(2)}, u32[]{:S(2)}) async-start(f32[16,8,128,8]{2,3,1,0:T(8,128)} %stack.21), calls=%async_computation.6 | async-start | bytes 1048576 | tf_op jit(solution)/shard_map/all_to_all | solution.py:182
  425.1 0.8 copy-start.4
  429.2 3.7 copy-start.1
  453.5 3.7 copy-start.1
  477.8 3.7 copy-start.1
  502.1 3.7 copy-start.1
  526.4 3.7 copy-start.1
  550.7 3.7 copy-start.1
  635.5 11.6 %collective-permute-start.12 = (bf16[3,4,8,64]{1,2,3,0:T(8,128)(2,1)}, bf16[3,4,8,64]{1,2,3,0:T(8,128)(2,1)}, u32[]{:S(2)}, u32[]{:S(2)}) collective-permute-start(bf16[3,4,8,64]{1,2,3,0:T(8,128)(2,1)} %get-tuple-element.515), channel_id=1, source_target_pairs={{0,16},{16,32},{32,48},{48,64},{64,80},{80,96},{96,112},{1,17},{17... | collective-permute-start | bytes 36872 | tf_op jit(solution)/shard_map/ppermute | solution.py:23
  639.0 13.2 %collective-permute-start.13 = (bf16[3,4,8,64]{1,2,3,0:T(8,128)(2,1)}, bf16[3,4,8,64]{1,2,3,0:T(8,128)(2,1)S(1)}, u32[]{:S(2)}, u32[]{:S(2)}) collective-permute-start(bf16[3,4,8,64]{1,2,3,0:T(8,128)(2,1)} %get-tuple-element.516), channel_id=1, source_target_pairs={{16,0},{32,16},{48,32},{64,48},{80,64},{96,80},{112,96},{17,1},{33... | collective-permute-start | bytes 36872 | tf_op jit(solution)/shard_map/ppermute | solution.py:25
  652.7 12.6 %collective-permute-start.14 = (bf16[3,24,4,64]{3,2,1,0:T(4,128)(2,1)S(1)}, bf16[3,24,4,64]{3,2,1,0:T(4,128)(2,1)S(1)}, u32[]{:S(2)}, u32[]{:S(2)}) collective-permute-start(bf16[3,24,4,64]{3,2,1,0:T(4,128)(2,1)S(1)} %get-tuple-element.517), channel_id=1, source_target_pairs={{0,1},{1,2},{2,3},{3,4},{4,5},{5,6},{6,7},{7,8},{8,9},{9,10},{10,1... | collective-permute-start | bytes 110600 | tf_op jit(solution)/shard_map/ppermute | solution.py:23
  659.1 9.3 %collective-permute-start.15 = (bf16[3,24,4,64]{3,2,1,0:T(4,128)(2,1)S(1)}, bf16[3,24,4,64]{3,2,1,0:T(4,128)(2,1)S(1)}, u32[]{:S(2)}, u32[]{:S(2)}) collective-permute-start(bf16[3,24,4,64]{3,2,1,0:T(4,128)(2,1)S(1)} %get-tuple-element.518), channel_id=1, source_target_pairs={{1,0},{2,1},{3,2},{4,3},{5,4},{6,5},{7,6},{8,7},{9,8},{10,9},{11,1... | collective-permute-start | bytes 110600 | tf_op jit(solution)/shard_map/ppermute | solution.py:25
  671.4 1.0 copy-start.3
